TPU v7x, 32 devices: a whole 2x2x4 slice. The times are simulated.
32 devices in a mesh: gx: 2 (over core), gy: 16 (over z, y, x).
Axes of the slice: x: 2, y: 2, z: 4, core: 2. Of those that a mesh axis runs over, the one named last changes fastest.
Arguments:
- density: float32 [32, 256, 256], P('gx', 'gy'), may hold values from 0.5 to 2
- momentum: float32 [3, 32, 256, 256], P(None, 'gx', 'gy'), may hold values from -3 to 3
- energy: float32 [32, 256, 256], P('gx', 'gy'), may hold values from 1 to 3
- parcel_mass: float32 [262144], P(('gx', 'gy')), may hold values from 0.2 to 2
- droplet_velocity: float32 [3, 262144], P(None, ('gx', 'gy')), may hold values from -4 to 4
- parcel_temp: float32 [262144], P(('gx', 'gy')), may hold values from 0.1 to 4
- parcel_cell: int32 [3, 262144], P(None, ('gx', 'gy')), may hold values from 0 to 255, as said below
- parcel_count: int32 [32], P(('gx', 'gy')), may hold values from 2048 to 8192, as said below
Outputs:
- updated_fluid_density: float32 [32, 256, 256], P('gx', 'gy')
- updated_fluid_impulse: float32 [3, 32, 256, 256], P(None, 'gx', 'gy')
- energy_out: float32 [32, 256, 256], P('gx', 'gy')
- moved_state: float32 [5, 327680], P(None, ('gx', 'gy'))
- moved_cell: int32 [3, 327680], P(None, ('gx', 'gy'))
- time_step: float32 [], replicated
Inputs may be any that keep to these rules, and one draw needn't show every extreme that they name: `parcel_cell`: each row of device d lies in d's block of 16 x 16 x 256 cells or in the layer of cells just beyond one of its four side faces inside the grid, never beyond an edge. Among the live rows of one device at most 512 lie beyond any one face; on every device some face along each of the two axes has exactly 512. `parcel_count`: some devices are full.
All inputs are finite; a program needn't handle non-finite values.
Results may differ from a plain program's by a relative error of at most 0.0003.
Values sent between devices are 32-bit elements; how exact they have to be, the bound alone decides.
A program may use at most 192 MiB of HBM per device.

v0:
```python
import functools

import jax
import jax.numpy as jnp
from jax import lax
from jax.experimental import pallas as pl
from jax.experimental.pallas import tpu as pltpu
from jax.sharding import PartitionSpec as P

ADIABATIC_INDEX = 1.4
KICK = 0.25
COURANT = 0.4
SHRINK = 0.5
MESH = pl.DeviceIdType.MESH
CHUNK = 1024
F32 = jnp.float32
BF16 = jnp.bfloat16
F8 = jnp.float8_e4m3fn
LIFT = 2048.0


def dot_nt(a, b):
    return lax.dot_general(a, b, (((1,), (1,)), ((), ())), preferred_element_type=F32)


def two_terms(x):
    high = x.astype(BF16)
    low = (x - high.astype(F32)).astype(BF16)
    return high, low


def one_hot_rows(row, count):
    lanes = row.shape[1]
    base = (
        jnp.broadcast_to(row, (16, lanes))
        - lax.broadcasted_iota(jnp.int32, (16, lanes), 0).astype(F32)
    ).astype(BF16)
    one, zero = jnp.ones((16, lanes), BF16), jnp.zeros((16, lanes), BF16)
    return jnp.concatenate(
        [jnp.where(base == 16.0 * k, one, zero) for k in range(count // 16)], axis=0
    )


def kernel(
    n_gx, n_gy, count_ref, density_hbm, momentum_hbm, energy_hbm, mass_hbm, vel_hbm, temp_hbm, cell_hbm,
    rho_ref, imp_ref, en_ref, state_ref, moved_ref, step_ref,
    src_ref, pay_ref, col_ref, q_ref, r_ref, a0_ref, a1_ref, b0_ref, b1_ref, c0_ref, c1_ref, d0_ref, d1_ref, acc_ref, low_ref, small_ref,
    out_bucket, in_bucket, out_face, in_face, max_x, max_y,
    bucket_send, bucket_recv, face_send, face_recv, mx_send, mx_recv, my_send, my_recv,
    density_ref, momentum_ref, energy_ref, mass_ref, vel_ref, temp_ref, cell_ref, load_sem,
):
    sources = (mass_hbm, temp_hbm, vel_hbm, cell_hbm, energy_hbm, density_hbm, momentum_hbm)
    places = (mass_ref, temp_ref, vel_ref, cell_ref, energy_ref, density_ref, momentum_ref)
    loads = []
    for k in range(7):
        load = pltpu.make_async_copy(sources[k], places[k], load_sem.at[k])
        load.start()
        loads.append(load)
    gx, gy = lax.axis_index("gx"), lax.axis_index("gy")
    cx, cy, nz = density_ref.shape
    rows = mass_ref.shape[1]
    cap = rows // 16
    per = cap // 128

    barrier = pltpu.get_barrier_semaphore()
    for k in range(1, n_gx):
        pl.semaphore_signal(barrier, inc=1, device_id={"gx": lax.rem(gx + k, n_gx)}, device_id_type=MESH)
    for k in range(1, n_gy):
        pl.semaphore_signal(barrier, inc=1, device_id={"gy": lax.rem(gy + k, n_gy)}, device_id_type=MESH)

    for load in loads[:4]:
        load.wait()
    mass, temp = mass_ref[...], temp_ref[...]
    live = lax.broadcasted_iota(jnp.int32, (1, rows), 1) < count_ref[0]
    evap = jnp.where(live, mass * jax.nn.sigmoid(2.0 * (temp - 2.0)), 0.0)
    vx, vy, vz = vel_ref[0:1, :], vel_ref[1:2, :], vel_ref[2:3, :]
    src_ref[0:1, :] = evap
    src_ref[1:2, :] = evap * vx
    src_ref[2:3, :] = evap * vy
    src_ref[3:4, :] = evap * vz
    src_ref[4:5, :] = evap * (temp + 0.5 * (vx * vx + vy * vy + vz * vz))
    pay_ref[0:1, :] = mass - SHRINK * evap
    pay_ref[1:4, :] = vel_ref[...]
    pay_ref[4:5, :] = temp
    pay_ref[5:8, :] = cell_ref[...].astype(F32)
    lx = cell_ref[0:1, :] - gx * cx
    ly = cell_ref[1:2, :] - gy * cy
    heading = jnp.where(
        lx < 0, 0, jnp.where(lx >= cx, 1, jnp.where(ly < 0, 2, jnp.where(ly >= cy, 3, 4)))
    )
    heading = jnp.where(live, heading, 5)
    stays = heading == 4
    col_ref[...] = jnp.where(stays, lx * cy + ly, -1000).astype(F32)
    state_ref[:, :rows] = jnp.where(stays, pay_ref[0:5, :], 0.0)
    moved_ref[:, :rows] = jnp.where(stays, cell_ref[...], 0)

    blocks = rows // 128
    marks = jnp.where(
        jnp.broadcast_to(heading, (8, rows)) == lax.broadcasted_iota(jnp.int32, (8, rows), 0), 1.0, 0.0
    )
    stacked = jnp.concatenate([marks[:, k * 128 : (k + 1) * 128] for k in range(blocks)], axis=0)
    i0 = lax.broadcasted_iota(jnp.int32, (128, 256), 0)
    i1 = lax.broadcasted_iota(jnp.int32, (128, 256), 1)
    upper = jnp.where((i0 < i1) | (i1 >= 128), 1.0, 0.0).astype(BF16)
    sums = jnp.dot(stacked.astype(BF16), upper, preferred_element_type=F32)
    carry = jnp.zeros((8, 128), F32)
    ranks = []
    for k in range(blocks):
        part = sums[k * 8 : (k + 1) * 8]
        mark = stacked[k * 8 : (k + 1) * 8]
        ranks.append(jnp.sum((part[:, :128] + carry) * mark, axis=0, keepdims=True))
        carry = carry + part[:, 128:]
    rank = jnp.concatenate(ranks, axis=1).astype(jnp.int32)
    q_ref[...] = jnp.where(heading < 4, heading * per + (rank >> 7), -1).astype(F32)
    r_ref[...] = (rank & 127).astype(F32)

    groups = 4 * per
    small_ref[...] = jnp.zeros_like(small_ref)

    def pack(c, carry):
        lanes = pl.ds(pl.multiple_of(c * CHUNK, CHUNK), CHUNK)
        high, low = two_terms(pay_ref[:, lanes])
        both = jnp.concatenate([high.astype(F32), low.astype(F32)], axis=0).astype(BF16)
        q = jnp.broadcast_to(q_ref[:, lanes], (16, CHUNK)).astype(BF16)
        zero = jnp.zeros((16, CHUNK), BF16)
        left = jnp.concatenate([jnp.where(q == float(k), both, zero) for k in range(groups)], axis=0)
        small_ref[...] += dot_nt(left, one_hot_rows(r_ref[:, lanes], 128))
        return carry

    lax.fori_loop(0, rows // CHUNK, pack, 0)
    for h in range(4):
        for j in range(per):
            k = (h * per + j) * 16
            out_bucket[h, :, j * 128 : (j + 1) * 128] = small_ref[k : k + 8, :] + small_ref[k + 8 : k + 16, :]

    pl.semaphore_wait(barrier, n_gx - 1 + n_gy - 1)

    targets = (
        {"gx": lax.rem(gx + n_gx - 1, n_gx)},
        {"gx": lax.rem(gx + 1, n_gx)},
        {"gy": lax.rem(gy + n_gy - 1, n_gy)},
        {"gy": lax.rem(gy + 1, n_gy)},
    )
    landing = (1, 0, 3, 2)

    def exchange(src, dst, send, recv):
        copies = []
        for h in range(4):
            copy = pltpu.make_async_remote_copy(
                src_ref=src.at[h], dst_ref=dst.at[landing[h]], send_sem=send.at[h],
                recv_sem=recv.at[landing[h]], device_id=targets[h], device_id_type=MESH,
            )
            copy.start()
            copies.append(copy)
        return copies

    moves = exchange(out_bucket, in_bucket, bucket_send, bucket_recv)

    cells = cx * cy
    acc_ref[...] = jnp.zeros_like(acc_ref)
    low_ref[...] = jnp.zeros_like(low_ref)

    def build(c, a_ref, b_ref, c_ref, d_ref):
        lanes = pl.ds(pl.multiple_of(c * CHUNK, CHUNK), CHUNK)
        base = (
            jnp.broadcast_to(col_ref[:, lanes], (16, CHUNK))
            - lax.broadcasted_iota(jnp.int32, (16, CHUNK), 0).astype(F32)
        ).astype(BF16)
        zero = jnp.zeros((16, CHUNK), BF16)
        hits = [base == 16.0 * k for k in range(cells // 16)]
        for v in range(5):
            value = jnp.broadcast_to(src_ref[v : v + 1, lanes], (16, CHUNK))
            high, low = two_terms(value)
            low = ((value - high.astype(F32)) * LIFT).astype(BF16)
            for k in range(cells // 16):
                at = v * cells + k * 16
                a_ref[at : at + 16, :] = jnp.where(hits[k], high, zero)
            for k in range(0, cells // 16, 2):
                at = v * cells + k * 16
                pair = jnp.concatenate([jnp.where(hits[k], low, zero), jnp.where(hits[k + 1], low, zero)], axis=0)
                c_ref[at : at + 32, :] = pair.astype(F8)
        depth = one_hot_rows(cell_ref[2:3, lanes].astype(F32), nz)
        b_ref[...] = depth
        d_ref[...] = depth.astype(F8)

    chunks = rows // CHUNK
    build(0, a0_ref, b0_ref, c0_ref, d0_ref)

    def two_chunks(i, carry):
        acc_ref[...] += dot_nt(a0_ref[...], b0_ref[...])
        low_ref[...] += dot_nt(c0_ref[...], d0_ref[...])
        build(2 * i + 1, a1_ref, b1_ref, c1_ref, d1_ref)
        acc_ref[...] += dot_nt(a1_ref[...], b1_ref[...])
        low_ref[...] += dot_nt(c1_ref[...], d1_ref[...])
        build(jnp.minimum(2 * i + 2, chunks - 1), a0_ref, b0_ref, c0_ref, d0_ref)
        return carry

    lax.fori_loop(0, chunks // 2, two_chunks, 0)

    acc_ref[...] += low_ref[...] * (1.0 / LIFT)

    for copy in moves:
        copy.wait_recv()
    for b in range(4):
        got = in_bucket[b]
        state_ref[:, rows + b * cap : rows + (b + 1) * cap] = got[0:5]
        moved_ref[:, rows + b * cap : rows + (b + 1) * cap] = got[5:8].astype(jnp.int32)
        warm = got[4:5]
        share = jax.nn.sigmoid(2.0 * (warm - 2.0))
        boiled = got[0:1] * share / (1.0 - SHRINK * share)
        speed = got[1:4]
        budget = 0.5 * jnp.sum(speed * speed, axis=0, keepdims=True)
        values = [boiled] + [boiled * got[k : k + 1] for k in (1, 2, 3)] + [boiled * (warm + budget)]
        if b < 2:
            along = got[6:7] - (gy * cy).astype(F32)
        else:
            along = got[5:6] - (gx * cx).astype(F32)
        hit = (
            jnp.broadcast_to(along, (16, cap))
            == lax.broadcasted_iota(jnp.int32, (16, cap), 0).astype(F32)
        )
        parts = []
        for value in values:
            wide = jnp.where(hit, jnp.broadcast_to(value, (16, cap)), 0.0)
            parts.append(two_terms(wide))
        left = jnp.concatenate([p[0] for p in parts] + [p[1] for p in parts], axis=0)
        depth = one_hot_rows(got[7:8], nz)
        sums = dot_nt(left, depth)
        sums = sums[0 : 5 * 16] + sums[5 * 16 : 10 * 16]
        for v in range(5):
            part = sums[v * 16 : (v + 1) * 16]
            if b < 2:
                at = v * cells + (0 if b == 0 else (cx - 1) * cy)
                acc_ref[at : at + cy, :] += part
            else:
                edge = 0 if b == 2 else cy - 1
                for x in range(cx):
                    at = v * cells + x * cy + edge
                    acc_ref[at : at + 1, :] += part[x : x + 1]

    def deposit(v):
        return acc_ref[v * cells : (v + 1) * cells, :].reshape(cx, cy, nz)

    for load in loads[4:]:
        load.wait()
    energy = energy_ref[...] + deposit(4)
    en_ref[...] = energy
    pressure = (ADIABATIC_INDEX - 1.0) * energy
    out_face[0] = pressure[0]
    out_face[1] = pressure[cx - 1]
    for x in range(cx):
        out_face[2, x : x + 1, :] = pressure[x, 0:1, :]
        out_face[3, x : x + 1, :] = pressure[x, cy - 1 : cy, :]
    faces = exchange(out_face, in_face, face_send, face_recv)

    density = density_ref[...] + deposit(0)
    rho_ref[...] = density
    lane = lax.broadcasted_iota(jnp.int32, (cx, cy, nz), 2)
    after = jnp.where(lane == nz - 1, 0.0, pltpu.roll(pressure, nz - 1, 2))
    before = jnp.where(lane == 0, 0.0, pltpu.roll(pressure, 1, 2))
    impulse_z = momentum_ref[2] + deposit(3) - KICK * (0.5 * (after - before))
    imp_ref[2] = impulse_z
    sound = jnp.sqrt(ADIABATIC_INDEX * pressure / density)
    for copy in faces:
        copy.wait_recv()
    low_x = jnp.where(gx > 0, in_face[0], 0.0)
    high_x = jnp.where(gx < n_gx - 1, in_face[1], 0.0)
    low_y = jnp.where(gy > 0, in_face[2], 0.0)
    high_y = jnp.where(gy < n_gy - 1, in_face[3], 0.0)
    after = jnp.concatenate([pressure[1:], high_x[None]], axis=0)
    before = jnp.concatenate([low_x[None], pressure[:-1]], axis=0)
    impulse_x = momentum_ref[0] + deposit(1) - KICK * (0.5 * (after - before))
    imp_ref[0] = impulse_x
    line = lax.broadcasted_iota(jnp.int32, (cx, cy, nz), 1)
    after = jnp.where(line == cy - 1, high_y[:, None, :], pltpu.roll(pressure, cy - 1, 1))
    before = jnp.where(line == 0, low_y[:, None, :], pltpu.roll(pressure, 1, 1))
    impulse_y = momentum_ref[1] + deposit(2) - KICK * (0.5 * (after - before))
    imp_ref[1] = impulse_y
    fastest = jnp.maximum(jnp.maximum(jnp.abs(impulse_x), jnp.abs(impulse_y)), jnp.abs(impulse_z))
    wave = fastest / density + sound

    def share_max(value, axis, me, n, slots, send, recv):
        slots[me] = jnp.broadcast_to(value, (8, 128))
        copies = []
        for k in range(1, n):
            copy = pltpu.make_async_remote_copy(
                src_ref=slots.at[me], dst_ref=slots.at[me], send_sem=send.at[k],
                recv_sem=recv.at[k], device_id={axis: lax.rem(me + k, n)}, device_id_type=MESH,
            )
            copy.start()
            copies.append(copy)
        for copy in copies:
            copy.wait_recv()
        best = jnp.max(slots[...])
        return best, copies

    top = jnp.max(jnp.max(wave, axis=(0, 1)))
    top, sent_x = share_max(top, "gx", gx, n_gx, max_x, mx_send, mx_recv)
    top, sent_y = share_max(top, "gy", gy, n_gy, max_y, my_send, my_recv)
    step_ref[...] = COURANT / jnp.broadcast_to(top, (1, 128))
    for copy in moves + faces + sent_x + sent_y:
        copy.wait_send()


def put_out(*refs):
    count = (len(refs) - 1) // 2
    copies = []
    for k in range(count):
        copy = pltpu.make_async_copy(refs[k], refs[count + k], refs[-1].at[k])
        copy.start()
        copies.append(copy)
    for copy in copies:
        copy.wait()


def on_device(n_gx, n_gy, density, momentum, energy, mass, velocity, temp, cell, count):
    rows = mass.shape[0]
    cap = rows // 16
    slots = rows + 4 * cap
    cx, cy, nz = density.shape
    vmem = pl.BlockSpec(memory_space=pltpu.VMEM)
    cells = cx * cy
    outs = pl.pallas_call(
        functools.partial(kernel, n_gx, n_gy),
        out_shape=(
            pltpu.VMEM(density.shape, F32),
            pltpu.VMEM(momentum.shape, F32),
            pltpu.VMEM(energy.shape, F32),
            pltpu.VMEM((5, slots), F32),
            pltpu.VMEM((3, slots), jnp.int32),
            pltpu.VMEM((1, 128), F32),
        ),
        in_specs=[pl.BlockSpec(memory_space=pltpu.SMEM)] + [pl.BlockSpec(memory_space=pltpu.HBM)] * 7,
        out_specs=(vmem,) * 6,
        scratch_shapes=[
            pltpu.VMEM((8, rows), F32),
            pltpu.VMEM((8, rows), F32),
            pltpu.VMEM((1, rows), F32),
            pltpu.VMEM((1, rows), F32),
            pltpu.VMEM((1, rows), F32),
            pltpu.VMEM((5 * cells, CHUNK), BF16),
            pltpu.VMEM((5 * cells, CHUNK), BF16),
            pltpu.VMEM((nz, CHUNK), BF16),
            pltpu.VMEM((nz, CHUNK), BF16),
            pltpu.VMEM((5 * cells, CHUNK), F8),
            pltpu.VMEM((5 * cells, CHUNK), F8),
            pltpu.VMEM((nz, CHUNK), F8),
            pltpu.VMEM((nz, CHUNK), F8),
            pltpu.VMEM((5 * cells, nz), F32),
            pltpu.VMEM((5 * cells, nz), F32),
            pltpu.VMEM((4 * (cap // 128) * 16, 128), F32),
            pltpu.VMEM((4, 8, cap), F32),
            pltpu.VMEM((4, 8, cap), F32),
            pltpu.VMEM((4, cx, nz), F32),
            pltpu.VMEM((4, cx, nz), F32),
            pltpu.VMEM((n_gx, 8, 128), F32),
            pltpu.VMEM((n_gy, 8, 128), F32),
            pltpu.SemaphoreType.DMA((4,)),
            pltpu.SemaphoreType.DMA((4,)),
            pltpu.SemaphoreType.DMA((4,)),
            pltpu.SemaphoreType.DMA((4,)),
            pltpu.SemaphoreType.DMA((n_gx,)),
            pltpu.SemaphoreType.DMA((n_gx,)),
            pltpu.SemaphoreType.DMA((n_gy,)),
            pltpu.SemaphoreType.DMA((n_gy,)),
            pltpu.VMEM(density.shape, F32),
            pltpu.VMEM(momentum.shape, F32),
            pltpu.VMEM(energy.shape, F32),
            pltpu.VMEM((1, rows), F32),
            pltpu.VMEM(velocity.shape, F32),
            pltpu.VMEM((1, rows), F32),
            pltpu.VMEM(cell.shape, jnp.int32),
            pltpu.SemaphoreType.DMA((7,)),
        ],
        compiler_params=pltpu.CompilerParams(
            collective_id=0, has_side_effects=True, vmem_limit_bytes=64200000
        ),
        name="spray",
    )(count, density, momentum, energy, mass.reshape(1, rows), velocity, temp.reshape(1, rows), cell)
    final = pl.pallas_call(
        put_out,
        out_shape=tuple(pltpu.HBM(o.shape, o.dtype) for o in outs[:5]),
        in_specs=[vmem] * 5,
        out_specs=(pl.BlockSpec(memory_space=pltpu.HBM),) * 5,
        scratch_shapes=[pltpu.SemaphoreType.DMA((5,))],
        compiler_params=pltpu.CompilerParams(vmem_limit_bytes=8 * 1024 * 1024),
        name="put_out",
    )(*outs[:5])
    return tuple(final) + (outs[5][0, 0],)


def solution(mesh):
    in_specs = (
        P("gx", "gy", None),
        P(None, "gx", "gy", None),
        P("gx", "gy", None),
        P(("gx", "gy")),
        P(None, ("gx", "gy")),
        P(("gx", "gy")),
        P(None, ("gx", "gy")),
        P(("gx", "gy")),
    )
    out_specs = (
        P("gx", "gy", None),
        P(None, "gx", "gy", None),
        P("gx", "gy", None),
        P(None, ("gx", "gy")),
        P(None, ("gx", "gy")),
        P(),
    )
    return jax.shard_map(
        functools.partial(on_device, mesh.shape["gx"], mesh.shape["gy"]),
        mesh=mesh, in_specs=in_specs, out_specs=out_specs, check_vma=False,
    )
```

profile of v0, /device:TPU:0, one launch (start us, length us, event | category | flops | bytes accessed | tf_op | source)
XLA Modules:
  0.0 31.8 jit_solution(17579709236469295882)
XLA Ops:
  1.3 28.1 %spray.1 = (f32[16,16,256]{2,1,0:T(8,128)S(1)}, f32[3,16,16,256]{3,2,1,0:T(8,128)S(1)}, f32[16,16,256]{2,1,0:T(8,128)S(1)}, f32[5,10240]{1,0:T(8,128)S(1)}, s32[...) custom-call(s32[1]{0:T(128)S(6)} %copy.15.count_ref, f32[16,16,256]{2,1,0:T(8,128)} %density_hbm.1, ...), custom_call_target="tpu_custom_call" | custom-call | tf_op jit(solution)/shard_map/spray/pallas_call | solution.py:323
  29.4 1.3 %put_out.1 = (f32[16,16,256]{2,1,0:T(8,128)}, f32[3,16,16,256]{3,2,1,0:T(8,128)}, f32[16,16,256]{2,1,0:T(8,128)}, f32[5,10240]{1,0:T(8,128)}, s32[3,10240]{1,0:T(4,128)}) custom-call(f32[16,16,256]{2,1,0:T(8,128)S(1)} %get-tuple-element.17.refs_0_, f32[3,16,16,256]{3,2,1,0:T(8,128)S(1)} %get-tuple-element.18.refs_1_, ...), custom_call_target="tpu_custom_call" | custom-call | tf_op jit(solution)/shard_map/put_out/pallas_call | solution.py:380
where the time goes:
time: 32 us; the launch traced here: 31.8 us
  Pallas kernels  29.4 us (92%)
  between operations  2.45 us (8%)
    pallas_call x1, Pallas kernels, on_device(): pl.pallas_call(functools.partial(kernel, n_gx, n_gy), out_shape=(pltpu.VM...  28.1 us
    pallas_call x1, Pallas kernels, on_device(): pl.pallas_call(put_out, out_shape=tuple((pltpu.HBM(o.shape, o.dtype) for...  1.25 us

commit v1 on v0

v1 whole, which is shorter than its diff:
```python
import functools

import jax
import jax.numpy as jnp
from jax import lax
from jax.experimental import pallas as pl
from jax.experimental.pallas import tpu as pltpu
from jax.sharding import PartitionSpec as P

ADIABATIC_INDEX = 1.4
KICK = 0.25
COURANT = 0.4
SHRINK = 0.5
MESH = pl.DeviceIdType.MESH
CHUNK = 1024
F32 = jnp.float32
BF16 = jnp.bfloat16
F8 = jnp.float8_e4m3fn
LIFT = 512.0
EDGES_AT = 2


def dot_nt(a, b):
    return lax.dot_general(a, b, (((1,), (1,)), ((), ())), preferred_element_type=F32)


def two_terms(x):
    high = x.astype(BF16)
    low = (x - high.astype(F32)).astype(BF16)
    return high, low


def one_hot_rows(row, count):
    lanes = row.shape[1]
    base = (
        jnp.broadcast_to(row, (16, lanes))
        - lax.broadcasted_iota(jnp.int32, (16, lanes), 0).astype(F32)
    ).astype(BF16)
    one, zero = jnp.ones((16, lanes), BF16), jnp.zeros((16, lanes), BF16)
    return jnp.concatenate(
        [jnp.where(base == 16.0 * k, one, zero) for k in range(count // 16)], axis=0
    )


def peers_of(n_gx, n_gy):
    both = [(a, b) for a in range(n_gx) for b in range(n_gy) if a or b]
    if n_gx * n_gy <= 64:
        return (both,)
    return ([p for p in both if p[1] == 0], [p for p in both if p[0] == 0])


def kernel(
    n_gx, n_gy, count_ref, density_hbm, momentum_hbm, energy_hbm, mass_hbm, vel_hbm, temp_hbm, cell_hbm,
    rho_ref, imp_ref, en_ref, state_ref, moved_ref, step_ref,
    src_ref, pay_ref, col_ref, q_ref, r_ref, a0_ref, a1_ref, c0_ref, c1_ref, b_ref, d_ref, small_ref, inv_ref, sound_ref,
    out_bucket, in_bucket, out_face, in_face,
    bucket_send, bucket_recv, face_send, face_recv, max_send, max_recv,
    mass_ref, vel_ref, temp_ref, cell_ref, load_sem, *slots_refs,
):
    sources = (mass_hbm, temp_hbm, vel_hbm, cell_hbm, energy_hbm, density_hbm, momentum_hbm)
    places = (mass_ref, temp_ref, vel_ref, cell_ref, en_ref, rho_ref, imp_ref)
    loads = []
    for k in range(7):
        load = pltpu.make_async_copy(sources[k], places[k], load_sem.at[k])
        load.start()
        loads.append(load)
    gx, gy = lax.axis_index("gx"), lax.axis_index("gy")
    cx, cy, nz = rho_ref.shape
    rows = mass_ref.shape[1]
    cap = rows // 16
    per = cap // 128
    cells = cx * cy
    chunks = rows // CHUNK
    in_bucket[...] = jnp.zeros_like(in_bucket)
    in_face[...] = jnp.zeros_like(in_face)

    def peer(a, b):
        return {"gx": lax.rem(gx + a, n_gx), "gy": lax.rem(gy + b, n_gy)}

    rounds = peers_of(n_gx, n_gy)
    greeted = [p for group in rounds for p in group]
    barrier = pltpu.get_barrier_semaphore()
    for p in greeted:
        pl.semaphore_signal(barrier, inc=1, device_id=peer(*p), device_id_type=MESH)

    for load in loads[:4]:
        load.wait()
    mass, temp = mass_ref[...], temp_ref[...]
    live = lax.broadcasted_iota(jnp.int32, (1, rows), 1) < count_ref[0]
    evap = jnp.where(live, mass * jax.nn.sigmoid(2.0 * (temp - 2.0)), 0.0)
    vx, vy, vz = vel_ref[0:1, :], vel_ref[1:2, :], vel_ref[2:3, :]
    src_ref[0:1, :] = evap
    src_ref[1:2, :] = evap * vx
    src_ref[2:3, :] = evap * vy
    src_ref[3:4, :] = evap * vz
    src_ref[4:5, :] = evap * (temp + 0.5 * (vx * vx + vy * vy + vz * vz))
    pay_ref[0:1, :] = mass - SHRINK * evap
    pay_ref[1:4, :] = vel_ref[...]
    pay_ref[4:5, :] = temp
    pay_ref[5:8, :] = cell_ref[...].astype(F32)
    lx = cell_ref[0:1, :] - gx * cx
    ly = cell_ref[1:2, :] - gy * cy
    heading = jnp.where(
        lx < 0, 0, jnp.where(lx >= cx, 1, jnp.where(ly < 0, 2, jnp.where(ly >= cy, 3, 4)))
    )
    heading = jnp.where(live, heading, 5)
    stays = heading == 4
    col_ref[...] = jnp.where(stays, lx * cy + ly, -1000).astype(F32)
    state_ref[:, :rows] = jnp.where(stays, pay_ref[0:5, :], 0.0)
    moved_ref[:, :rows] = jnp.where(stays, cell_ref[...], 0)

    blocks = rows // 128
    marks = jnp.where(
        jnp.broadcast_to(heading, (8, rows)) == lax.broadcasted_iota(jnp.int32, (8, rows), 0), 1.0, 0.0
    )
    stacked = jnp.concatenate([marks[:, k * 128 : (k + 1) * 128] for k in range(blocks)], axis=0)
    i0 = lax.broadcasted_iota(jnp.int32, (128, 256), 0)
    i1 = lax.broadcasted_iota(jnp.int32, (128, 256), 1)
    upper = jnp.where((i0 < i1) | (i1 >= 128), 1.0, 0.0).astype(BF16)
    sums = jnp.dot(stacked.astype(BF16), upper, preferred_element_type=F32)
    carry = jnp.zeros((8, 128), F32)
    ranks = []
    for k in range(blocks):
        part = sums[k * 8 : (k + 1) * 8]
        mark = stacked[k * 8 : (k + 1) * 8]
        ranks.append(jnp.sum((part[:, :128] + carry) * mark, axis=0, keepdims=True))
        carry = carry + part[:, 128:]
    rank = jnp.concatenate(ranks, axis=1).astype(jnp.int32)
    q_ref[...] = jnp.where(heading < 4, heading * per + (rank >> 7), -1).astype(F32)
    r_ref[...] = (rank & 127).astype(F32)

    groups = 4 * per
    small_ref[...] = jnp.zeros_like(small_ref)

    def columns(lanes):
        base = (
            jnp.broadcast_to(col_ref[:, lanes], (16, CHUNK))
            - lax.broadcasted_iota(jnp.int32, (16, CHUNK), 0).astype(F32)
        ).astype(BF16)
        return [base == 16.0 * k for k in range(cells // 16)]

    def spread(v, lanes, hits):
        zero = jnp.zeros((16, CHUNK), BF16)
        value = jnp.broadcast_to(src_ref[v : v + 1, lanes], (16, CHUNK))
        high = value.astype(BF16)
        low = ((value - high.astype(F32)) * LIFT).astype(BF16)
        first = [jnp.where(hits[k], high, zero) for k in range(cells // 16)]
        second = [
            jnp.concatenate([jnp.where(hits[k], low, zero), jnp.where(hits[k + 1], low, zero)], axis=0).astype(F8)
            for k in range(0, cells // 16, 2)
        ]
        return first, second

    def front(c):
        lanes = pl.ds(pl.multiple_of(c * CHUNK, CHUNK), CHUNK)
        high, low = two_terms(pay_ref[:, lanes])
        both = jnp.concatenate([high.astype(F32), low.astype(F32)], axis=0).astype(BF16)
        q = jnp.broadcast_to(q_ref[:, lanes], (16, CHUNK)).astype(BF16)
        zero = jnp.zeros((16, CHUNK), BF16)
        left = jnp.concatenate([jnp.where(q == float(k), both, zero) for k in range(groups)], axis=0)
        small_ref[...] += dot_nt(left, one_hot_rows(r_ref[:, lanes], 128))
        depth = one_hot_rows(cell_ref[2:3, lanes].astype(F32), nz)
        unit = (depth * (1.0 / LIFT)).astype(F8)
        b_ref[c] = depth
        d_ref[c] = unit
        first, second = spread(4, lanes, columns(lanes))
        part = dot_nt(jnp.concatenate(first, axis=0), depth) + dot_nt(jnp.concatenate(second, axis=0), unit)
        en_ref[...] += part.reshape(cx, cy, nz)

    def two_front(i, carry):
        front(2 * i)
        front(2 * i + 1)
        return carry

    loads[4].wait()
    lax.fori_loop(0, chunks // 2, two_front, 0)
    for h in range(4):
        for j in range(per):
            k = (h * per + j) * 16
            out_bucket[h, :, j * 128 : (j + 1) * 128] = small_ref[k : k + 8, :] + small_ref[k + 8 : k + 16, :]

    def build(c, a_ref, c_ref):
        lanes = pl.ds(pl.multiple_of(c * CHUNK, CHUNK), CHUNK)
        hits = columns(lanes)
        for v in range(4):
            first, second = spread(v, lanes, hits)
            for k in range(cells // 16):
                at = v * cells + k * 16
                a_ref[at : at + 16, :] = first[k]
            for k in range(cells // 32):
                at = v * cells + k * 32
                c_ref[at : at + 32, :] = second[k]

    build(0, a0_ref, c0_ref)

    pl.semaphore_wait(barrier, len(greeted))

    targets = (
        {"gx": lax.rem(gx + n_gx - 1, n_gx)},
        {"gx": lax.rem(gx + 1, n_gx)},
        {"gy": lax.rem(gy + n_gy - 1, n_gy)},
        {"gy": lax.rem(gy + 1, n_gy)},
    )
    there = (gx > 0, gx < n_gx - 1, gy > 0, gy < n_gy - 1)
    landing = (1, 0, 3, 2)

    def link(h, src, dst, send, recv):
        return pltpu.make_async_remote_copy(
            src_ref=src.at[h], dst_ref=dst.at[landing[h]], send_sem=send.at[h],
            recv_sem=recv.at[landing[h]], device_id=targets[h], device_id_type=MESH,
        )

    def launch(*refs):
        for h in range(4):
            pl.when(there[h])(lambda h=h: link(h, *refs).start())

    def arrive(*refs):
        for h in range(4):
            pl.when(there[landing[h]])(lambda h=h: link(h, *refs).wait_recv())

    def depart(*refs):
        for h in range(4):
            pl.when(there[h])(lambda h=h: link(h, *refs).wait_send())

    moves = (out_bucket, in_bucket, bucket_send, bucket_recv)
    faces = (out_face, in_face, face_send, face_recv)
    launch(*moves)
    for load in loads[5:]:
        load.wait()

    def edges():
        arrive(*moves)
        for b in range(4):
            got = in_bucket[b]
            state_ref[:, rows + b * cap : rows + (b + 1) * cap] = got[0:5]
            moved_ref[:, rows + b * cap : rows + (b + 1) * cap] = got[5:8].astype(jnp.int32)
            warm = got[4:5]
            share = jax.nn.sigmoid(2.0 * (warm - 2.0))
            boiled = got[0:1] * share / (1.0 - SHRINK * share)
            speed = got[1:4]
            budget = 0.5 * jnp.sum(speed * speed, axis=0, keepdims=True)
            values = [boiled] + [boiled * got[k : k + 1] for k in (1, 2, 3)] + [boiled * (warm + budget)]
            if b < 2:
                along = got[6:7] - (gy * cy).astype(F32)
            else:
                along = got[5:6] - (gx * cx).astype(F32)
            hit = (
                jnp.broadcast_to(along, (16, cap))
                == lax.broadcasted_iota(jnp.int32, (16, cap), 0).astype(F32)
            )
            parts = []
            for value in values:
                wide = jnp.where(hit, jnp.broadcast_to(value, (16, cap)), 0.0)
                parts.append(two_terms(wide))
            left = jnp.concatenate([p[0] for p in parts] + [p[1] for p in parts], axis=0)
            sums = dot_nt(left, one_hot_rows(got[7:8], nz))
            sums = sums[0 : 5 * 16] + sums[5 * 16 : 10 * 16]
            fields = (rho_ref, imp_ref.at[0], imp_ref.at[1], imp_ref.at[2], en_ref)
            for v in range(5):
                part = sums[v * 16 : (v + 1) * 16]
                if b < 2:
                    x = 0 if b == 0 else cx - 1
                    fields[v][x] += part
                else:
                    y = 0 if b == 2 else cy - 1
                    for x in range(cx):
                        fields[v][x, y : y + 1, :] += part[x : x + 1]
        scale = ADIABATIC_INDEX - 1.0
        out_face[0] = scale * en_ref[0]
        out_face[1] = scale * en_ref[cx - 1]
        for x in range(cx):
            out_face[2, x : x + 1, :] = scale * en_ref[x, 0:1, :]
            out_face[3, x : x + 1, :] = scale * en_ref[x, cy - 1 : cy, :]
        launch(*faces)

    def add(c, a_ref, c_ref):
        part = dot_nt(a_ref[...], b_ref[c]) + dot_nt(c_ref[...], d_ref[c])
        rho_ref[...] += part[:cells].reshape(cx, cy, nz)
        imp_ref[...] += part[cells:].reshape(3, cx, cy, nz)

    def two_chunks(i, carry):
        pl.when(i == EDGES_AT)(edges)
        add(2 * i, a0_ref, c0_ref)
        build(2 * i + 1, a1_ref, c1_ref)
        add(2 * i + 1, a1_ref, c1_ref)
        build(jnp.minimum(2 * i + 2, chunks - 1), a0_ref, c0_ref)
        return carry

    lax.fori_loop(0, chunks // 2, two_chunks, 0)

    pressure = (ADIABATIC_INDEX - 1.0) * en_ref[...]
    inverse = 1.0 / rho_ref[...]
    inv_ref[...] = inverse
    sound_ref[...] = jnp.sqrt(ADIABATIC_INDEX * pressure * inverse)
    lane = lax.broadcasted_iota(jnp.int32, (cx, cy, nz), 2)
    after = jnp.where(lane == nz - 1, 0.0, pltpu.roll(pressure, nz - 1, 2))
    before = jnp.where(lane == 0, 0.0, pltpu.roll(pressure, 1, 2))
    half = 0.5 * KICK
    imp_ref[2] -= half * (after - before)
    line = lax.broadcasted_iota(jnp.int32, (cx, cy, nz), 1)
    after = jnp.where(line == cy - 1, 0.0, pltpu.roll(pressure, cy - 1, 1))
    before = jnp.where(line == 0, 0.0, pltpu.roll(pressure, 1, 1))
    imp_ref[1] -= half * (after - before)
    none = jnp.zeros((1, cy, nz), F32)
    after = jnp.concatenate([pressure[1:], none], axis=0)
    before = jnp.concatenate([none, pressure[:-1]], axis=0)
    imp_ref[0] -= half * (after - before)
    arrive(*faces)
    imp_ref[0, 0] += half * in_face[0]
    imp_ref[0, cx - 1] -= half * in_face[1]
    for x in range(cx):
        imp_ref[1, x, 0:1, :] += half * in_face[2, x : x + 1, :]
        imp_ref[1, x, cy - 1 : cy, :] -= half * in_face[3, x : x + 1, :]
    fastest = jnp.maximum(jnp.maximum(jnp.abs(imp_ref[0]), jnp.abs(imp_ref[1])), jnp.abs(imp_ref[2]))
    wave = fastest * inv_ref[...] + sound_ref[...]
    wave = jnp.max(wave.reshape(cells, nz), axis=0, keepdims=True)
    top = functools.reduce(jnp.maximum, [wave[:, k * 128 : (k + 1) * 128] for k in range(nz // 128)])

    def everyone(slots, sem):
        rest = slots.at[pl.ds(1, slots.shape[0] - 1)]
        return pltpu.make_async_copy(rest, rest, sem)

    for t, group in enumerate(rounds):
        slots = slots_refs[t]
        slots[0] = top
        for k, p in enumerate(group):
            pltpu.make_async_remote_copy(
                src_ref=slots.at[0], dst_ref=slots.at[k + 1], send_sem=max_send.at[t],
                recv_sem=max_recv.at[t], device_id=peer(*p), device_id_type=MESH,
            ).start()
        everyone(slots, max_recv.at[t]).wait()
        top = jnp.max(slots[...], axis=0)
    step_ref[...] = COURANT / jnp.broadcast_to(jnp.max(top, axis=1, keepdims=True), (1, 128))
    depart(*moves)
    depart(*faces)
    for t in range(len(rounds)):
        everyone(slots_refs[t], max_send.at[t]).wait()


def put_out(*refs):
    count = (len(refs) - 1) // 2
    copies = []
    for k in range(count):
        copy = pltpu.make_async_copy(refs[k], refs[count + k], refs[-1].at[k])
        copy.start()
        copies.append(copy)
    for copy in copies:
        copy.wait()


def on_device(n_gx, n_gy, density, momentum, energy, mass, velocity, temp, cell, count):
    rows = mass.shape[0]
    cap = rows // 16
    slots = rows + 4 * cap
    cx, cy, nz = density.shape
    vmem = pl.BlockSpec(memory_space=pltpu.VMEM)
    cells = cx * cy
    rounds = peers_of(n_gx, n_gy)
    outs = pl.pallas_call(
        functools.partial(kernel, n_gx, n_gy),
        out_shape=(
            pltpu.VMEM(density.shape, F32),
            pltpu.VMEM(momentum.shape, F32),
            pltpu.VMEM(energy.shape, F32),
            pltpu.VMEM((5, slots), F32),
            pltpu.VMEM((3, slots), jnp.int32),
            pltpu.VMEM((1, 128), F32),
        ),
        in_specs=[pl.BlockSpec(memory_space=pltpu.SMEM)] + [pl.BlockSpec(memory_space=pltpu.HBM)] * 7,
        out_specs=(vmem,) * 6,
        scratch_shapes=[
            pltpu.VMEM((8, rows), F32),
            pltpu.VMEM((8, rows), F32),
            pltpu.VMEM((1, rows), F32),
            pltpu.VMEM((1, rows), F32),
            pltpu.VMEM((1, rows), F32),
            pltpu.VMEM((4 * cells, CHUNK), BF16),
            pltpu.VMEM((4 * cells, CHUNK), BF16),
            pltpu.VMEM((4 * cells, CHUNK), F8),
            pltpu.VMEM((4 * cells, CHUNK), F8),
            pltpu.VMEM((rows // CHUNK, nz, CHUNK), BF16),
            pltpu.VMEM((rows // CHUNK, nz, CHUNK), F8),
            pltpu.VMEM((4 * (cap // 128) * 16, 128), F32),
            pltpu.VMEM(density.shape, F32),
            pltpu.VMEM(density.shape, F32),
            pltpu.VMEM((4, 8, cap), F32),
            pltpu.VMEM((4, 8, cap), F32),
            pltpu.VMEM((4, cx, nz), F32),
            pltpu.VMEM((4, cx, nz), F32),
            pltpu.SemaphoreType.DMA((4,)),
            pltpu.SemaphoreType.DMA((4,)),
            pltpu.SemaphoreType.DMA((4,)),
            pltpu.SemaphoreType.DMA((4,)),
            pltpu.SemaphoreType.DMA((len(rounds),)),
            pltpu.SemaphoreType.DMA((len(rounds),)),
            pltpu.VMEM((1, rows), F32),
            pltpu.VMEM(velocity.shape, F32),
            pltpu.VMEM((1, rows), F32),
            pltpu.VMEM(cell.shape, jnp.int32),
            pltpu.SemaphoreType.DMA((7,)),
        ] + [pltpu.VMEM((len(group) + 1, 1, 128), F32) for group in rounds],
        compiler_params=pltpu.CompilerParams(
            collective_id=0, has_side_effects=True, vmem_limit_bytes=64200000
        ),
        name="spray",
    )(count, density, momentum, energy, mass.reshape(1, rows), velocity, temp.reshape(1, rows), cell)
    final = pl.pallas_call(
        put_out,
        out_shape=tuple(pltpu.HBM(o.shape, o.dtype) for o in outs[:5]),
        in_specs=[vmem] * 5,
        out_specs=(pl.BlockSpec(memory_space=pltpu.HBM),) * 5,
        scratch_shapes=[pltpu.SemaphoreType.DMA((5,))],
        compiler_params=pltpu.CompilerParams(vmem_limit_bytes=8 * 1024 * 1024),
        name="put_out",
    )(*outs[:5])
    return tuple(final) + (outs[5][0, 0],)


def solution(mesh):
    in_specs = (
        P("gx", "gy", None),
        P(None, "gx", "gy", None),
        P("gx", "gy", None),
        P(("gx", "gy")),
        P(None, ("gx", "gy")),
        P(("gx", "gy")),
        P(None, ("gx", "gy")),
        P(("gx", "gy")),
    )
    out_specs = (
        P("gx", "gy", None),
        P(None, "gx", "gy", None),
        P("gx", "gy", None),
        P(None, ("gx", "gy")),
        P(None, ("gx", "gy")),
        P(),
    )
    return jax.shard_map(
        functools.partial(on_device, mesh.shape["gx"], mesh.shape["gy"]),
        mesh=mesh, in_specs=in_specs, out_specs=out_specs, check_vma=False,
    )
```

time: 32 us -> 27.1 us (0.85)
  Pallas kernels: 29.4 us -> 24.5 us
    pallas_call x1, Pallas kernels: 28.1 us -> 23.2 us  [on_device(): pl.pallas_call(functools.partial(kernel, n_gx, n_gy), out_shape=(pltpu.VM...]
where the time goes in v1:
time: 27.1 us; the launch traced here: 26.9 us
  Pallas kernels  24.5 us (90%)
  between operations  2.45 us (9%)
    pallas_call x1, Pallas kernels, on_device(): pl.pallas_call(functools.partial(kernel, n_gx, n_gy), out_shape=(pltpu.VM...  23.2 us
    pallas_call x1, Pallas kernels, on_device(): pl.pallas_call(put_out, out_shape=tuple((pltpu.HBM(o.shape, o.dtype) for...  1.25 us

profile of v1, /device:TPU:0, one launch (start us, length us, event | category | flops | bytes accessed | tf_op | source)
XLA Modules:
  0.0 26.9 jit_solution(5268701955496676439)
XLA Ops:
  1.3 23.2 %spray.1 = (f32[16,16,256]{2,1,0:T(8,128)S(1)}, f32[3,16,16,256]{3,2,1,0:T(8,128)S(1)}, f32[16,16,256]{2,1,0:T(8,128)S(1)}, f32[5,10240]{1,0:T(8,128)S(1)}, s32[...) custom-call(s32[1]{0:T(128)S(6)} %copy.15.count_ref, f32[16,16,256]{2,1,0:T(8,128)} %density_hbm.1, ...), custom_call_target="tpu_custom_call" | custom-call | tf_op jit(solution)/shard_map/spray/pallas_call | solution.py:359
  24.5 1.3 %put_out.1 = (f32[16,16,256]{2,1,0:T(8,128)}, f32[3,16,16,256]{3,2,1,0:T(8,128)}, f32[16,16,256]{2,1,0:T(8,128)}, f32[5,10240]{1,0:T(8,128)}, s32[3,10240]{1,0:T(4,128)}) custom-call(f32[16,16,256]{2,1,0:T(8,128)S(1)} %get-tuple-element.17.refs_0_, f32[3,16,16,256]{3,2,1,0:T(8,128)S(1)} %get-tuple-element.18.refs_1_, ...), custom_call_target="tpu_custom_call" | custom-call | tf_op jit(solution)/shard_map/put_out/pallas_call | solution.py:407

commit v2 on v1

--- a/solution.py
+++ b/solution.py
@@ -50,17 +50,17 @@
 
 
 def kernel(
-    n_gx, n_gy, count_ref, density_hbm, momentum_hbm, energy_hbm, mass_hbm, vel_hbm, temp_hbm, cell_hbm,
+    n_gx, n_gy, count_hbm, density_hbm, momentum_hbm, energy_hbm, mass_hbm, vel_hbm, temp_hbm, cell_hbm,
     rho_ref, imp_ref, en_ref, state_ref, moved_ref, step_ref,
-    src_ref, pay_ref, col_ref, q_ref, r_ref, a0_ref, a1_ref, c0_ref, c1_ref, b_ref, d_ref, small_ref, inv_ref, sound_ref,
+    upper_ref, src_ref, pay_ref, col_ref, q_ref, r_ref, a0_ref, a1_ref, c0_ref, c1_ref, b_ref, d_ref, small_ref, inv_ref, sound_ref,
     out_bucket, in_bucket, out_face, in_face,
     bucket_send, bucket_recv, face_send, face_recv, max_send, max_recv,
-    mass_ref, vel_ref, temp_ref, cell_ref, load_sem, *slots_refs,
+    count_ref, mass_ref, vel_ref, temp_ref, cell_ref, load_sem, *slots_refs,
 ):
-    sources = (mass_hbm, temp_hbm, vel_hbm, cell_hbm, energy_hbm, density_hbm, momentum_hbm)
-    places = (mass_ref, temp_ref, vel_ref, cell_ref, en_ref, rho_ref, imp_ref)
+    sources = (count_hbm, mass_hbm, temp_hbm, vel_hbm, cell_hbm, energy_hbm, density_hbm, momentum_hbm)
+    places = (count_ref, mass_ref, temp_ref, vel_ref, cell_ref, en_ref, rho_ref, imp_ref)
     loads = []
-    for k in range(7):
+    for k in range(8):
         load = pltpu.make_async_copy(sources[k], places[k], load_sem.at[k])
         load.start()
         loads.append(load)
@@ -83,51 +83,50 @@
     for p in greeted:
         pl.semaphore_signal(barrier, inc=1, device_id=peer(*p), device_id_type=MESH)
 
-    for load in loads[:4]:
+    for load in loads[:5]:
         load.wait()
-    mass, temp = mass_ref[...], temp_ref[...]
-    live = lax.broadcasted_iota(jnp.int32, (1, rows), 1) < count_ref[0]
-    evap = jnp.where(live, mass * jax.nn.sigmoid(2.0 * (temp - 2.0)), 0.0)
-    vx, vy, vz = vel_ref[0:1, :], vel_ref[1:2, :], vel_ref[2:3, :]
-    src_ref[0:1, :] = evap
-    src_ref[1:2, :] = evap * vx
-    src_ref[2:3, :] = evap * vy
-    src_ref[3:4, :] = evap * vz
-    src_ref[4:5, :] = evap * (temp + 0.5 * (vx * vx + vy * vy + vz * vz))
-    pay_ref[0:1, :] = mass - SHRINK * evap
-    pay_ref[1:4, :] = vel_ref[...]
-    pay_ref[4:5, :] = temp
-    pay_ref[5:8, :] = cell_ref[...].astype(F32)
-    lx = cell_ref[0:1, :] - gx * cx
-    ly = cell_ref[1:2, :] - gy * cy
-    heading = jnp.where(
-        lx < 0, 0, jnp.where(lx >= cx, 1, jnp.where(ly < 0, 2, jnp.where(ly >= cy, 3, 4)))
-    )
-    heading = jnp.where(live, heading, 5)
-    stays = heading == 4
-    col_ref[...] = jnp.where(stays, lx * cy + ly, -1000).astype(F32)
-    state_ref[:, :rows] = jnp.where(stays, pay_ref[0:5, :], 0.0)
-    moved_ref[:, :rows] = jnp.where(stays, cell_ref[...], 0)
-
-    blocks = rows // 128
-    marks = jnp.where(
-        jnp.broadcast_to(heading, (8, rows)) == lax.broadcasted_iota(jnp.int32, (8, rows), 0), 1.0, 0.0
-    )
-    stacked = jnp.concatenate([marks[:, k * 128 : (k + 1) * 128] for k in range(blocks)], axis=0)
+    blocks = CHUNK // 128
     i0 = lax.broadcasted_iota(jnp.int32, (128, 256), 0)
     i1 = lax.broadcasted_iota(jnp.int32, (128, 256), 1)
-    upper = jnp.where((i0 < i1) | (i1 >= 128), 1.0, 0.0).astype(BF16)
-    sums = jnp.dot(stacked.astype(BF16), upper, preferred_element_type=F32)
-    carry = jnp.zeros((8, 128), F32)
-    ranks = []
-    for k in range(blocks):
-        part = sums[k * 8 : (k + 1) * 8]
-        mark = stacked[k * 8 : (k + 1) * 8]
-        ranks.append(jnp.sum((part[:, :128] + carry) * mark, axis=0, keepdims=True))
-        carry = carry + part[:, 128:]
-    rank = jnp.concatenate(ranks, axis=1).astype(jnp.int32)
-    q_ref[...] = jnp.where(heading < 4, heading * per + (rank >> 7), -1).astype(F32)
-    r_ref[...] = (rank & 127).astype(F32)
+    upper_ref[...] = jnp.where((i0 < i1) | (i1 >= 128), 1.0, 0.0).astype(BF16)
+
+    def prepare(c, carry):
+        lanes = pl.ds(c * CHUNK, CHUNK)
+        mass, temp = mass_ref[:, lanes], temp_ref[:, lanes]
+        live = lax.broadcasted_iota(jnp.int32, (1, CHUNK), 1) + c * CHUNK < count_ref[0]
+        evap = jnp.where(live, mass * jax.nn.sigmoid(2.0 * (temp - 2.0)), 0.0)
+        vx, vy, vz = vel_ref[0:1, lanes], vel_ref[1:2, lanes], vel_ref[2:3, lanes]
+        src_ref[0:1, lanes] = evap
+        src_ref[1:2, lanes] = evap * vx
+        src_ref[2:3, lanes] = evap * vy
+        src_ref[3:4, lanes] = evap * vz
+        src_ref[4:5, lanes] = evap * (temp + 0.5 * (vx * vx + vy * vy + vz * vz))
+        pay_ref[0:1, lanes] = mass - SHRINK * evap
+        pay_ref[1:4, lanes] = vel_ref[:, lanes]
+        pay_ref[4:5, lanes] = temp
+        pay_ref[5:8, lanes] = cell_ref[:, lanes].astype(F32)
+        lx = cell_ref[0:1, lanes] - gx * cx
+        ly = cell_ref[1:2, lanes] - gy * cy
+        heading = jnp.where(
+            lx < 0, 0, jnp.where(lx >= cx, 1, jnp.where(ly < 0, 2, jnp.where(ly >= cy, 3, 4)))
+        )
+        heading = jnp.where(live, heading, 5)
+        col_ref[:, lanes] = jnp.where(heading == 4, lx * cy + ly, -1000).astype(F32)
+        marks = jnp.where(
+            jnp.broadcast_to(heading, (8, CHUNK)) == lax.broadcasted_iota(jnp.int32, (8, CHUNK), 0), 1.0, 0.0
+        )
+        stacked = jnp.concatenate([marks[:, k * 128 : (k + 1) * 128] for k in range(blocks)], axis=0)
+        sums = jnp.dot(stacked.astype(BF16), upper_ref[...], preferred_element_type=F32)
+        ranks = []
+        for k in range(blocks):
+            part = sums[k * 8 : (k + 1) * 8]
+            mark = stacked[k * 8 : (k + 1) * 8]
+            ranks.append(jnp.sum((part[:, :128] + carry) * mark, axis=0, keepdims=True))
+            carry = carry + part[:, 128:]
+        rank = jnp.concatenate(ranks, axis=1).astype(jnp.int32)
+        q_ref[:, lanes] = jnp.where(heading < 4, heading * per + (rank >> 7), -1).astype(F32)
+        r_ref[:, lanes] = (rank & 127).astype(F32)
+        return carry
 
     groups = 4 * per
     small_ref[...] = jnp.zeros_like(small_ref)
@@ -152,7 +151,7 @@
         return first, second
 
     def front(c):
-        lanes = pl.ds(pl.multiple_of(c * CHUNK, CHUNK), CHUNK)
+        lanes = pl.ds(c * CHUNK, CHUNK)
         high, low = two_terms(pay_ref[:, lanes])
         both = jnp.concatenate([high.astype(F32), low.astype(F32)], axis=0).astype(BF16)
         q = jnp.broadcast_to(q_ref[:, lanes], (16, CHUNK)).astype(BF16)
@@ -167,20 +166,21 @@
         part = dot_nt(jnp.concatenate(first, axis=0), depth) + dot_nt(jnp.concatenate(second, axis=0), unit)
         en_ref[...] += part.reshape(cx, cy, nz)
 
-    def two_front(i, carry):
-        front(2 * i)
-        front(2 * i + 1)
-        return carry
-
-    loads[4].wait()
-    lax.fori_loop(0, chunks // 2, two_front, 0)
+    count = jnp.zeros((8, 128), F32)
+    count = prepare(0, count)
+    count = prepare(1, count)
+    loads[5].wait()
+    for c in range(chunks):
+        if c + 2 < chunks:
+            count = prepare(c + 2, count)
+        front(c)
     for h in range(4):
         for j in range(per):
             k = (h * per + j) * 16
             out_bucket[h, :, j * 128 : (j + 1) * 128] = small_ref[k : k + 8, :] + small_ref[k + 8 : k + 16, :]
 
     def build(c, a_ref, c_ref):
-        lanes = pl.ds(pl.multiple_of(c * CHUNK, CHUNK), CHUNK)
+        lanes = pl.ds(c * CHUNK if isinstance(c, int) else pl.multiple_of(c * CHUNK, CHUNK), CHUNK)
         hits = columns(lanes)
         for v in range(4):
             first, second = spread(v, lanes, hits)
@@ -225,15 +225,13 @@
     moves = (out_bucket, in_bucket, bucket_send, bucket_recv)
     faces = (out_face, in_face, face_send, face_recv)
     launch(*moves)
-    for load in loads[5:]:
+    for load in loads[6:]:
         load.wait()
 
     def edges():
         arrive(*moves)
         for b in range(4):
             got = in_bucket[b]
-            state_ref[:, rows + b * cap : rows + (b + 1) * cap] = got[0:5]
-            moved_ref[:, rows + b * cap : rows + (b + 1) * cap] = got[5:8].astype(jnp.int32)
             warm = got[4:5]
             share = jax.nn.sigmoid(2.0 * (warm - 2.0))
             boiled = got[0:1] * share / (1.0 - SHRINK * share)
@@ -278,33 +276,45 @@
         rho_ref[...] += part[:cells].reshape(cx, cy, nz)
         imp_ref[...] += part[cells:].reshape(3, cx, cy, nz)
 
+    half = 0.5 * KICK
+
+    def kick():
+        pressure = (ADIABATIC_INDEX - 1.0) * en_ref[...]
+        lane = lax.broadcasted_iota(jnp.int32, (cx, cy, nz), 2)
+        after = jnp.where(lane == nz - 1, 0.0, pltpu.roll(pressure, nz - 1, 2))
+        before = jnp.where(lane == 0, 0.0, pltpu.roll(pressure, 1, 2))
+
+        imp_ref[2] -= half * (after - before)
+        line = lax.broadcasted_iota(jnp.int32, (cx, cy, nz), 1)
+        after = jnp.where(line == cy - 1, 0.0, pltpu.roll(pressure, cy - 1, 1))
+        before = jnp.where(line == 0, 0.0, pltpu.roll(pressure, 1, 1))
+        imp_ref[1] -= half * (after - before)
+        none = jnp.zeros((1, cy, nz), F32)
+        after = jnp.concatenate([pressure[1:], none], axis=0)
+        before = jnp.concatenate([none, pressure[:-1]], axis=0)
+        imp_ref[0] -= half * (after - before)
+
     def two_chunks(i, carry):
-        pl.when(i == EDGES_AT)(edges)
         add(2 * i, a0_ref, c0_ref)
         build(2 * i + 1, a1_ref, c1_ref)
         add(2 * i + 1, a1_ref, c1_ref)
-        build(jnp.minimum(2 * i + 2, chunks - 1), a0_ref, c0_ref)
+        build(2 * i + 2, a0_ref, c0_ref)
         return carry
 
-    lax.fori_loop(0, chunks // 2, two_chunks, 0)
-
-    pressure = (ADIABATIC_INDEX - 1.0) * en_ref[...]
+    head = EDGES_AT
+    lax.fori_loop(0, head, two_chunks, 0)
+    edges()
+    for c in range(2 * head, chunks):
+        a_ref, c_ref = ((a0_ref, c0_ref), (a1_ref, c1_ref))[c % 2]
+        add(c, a_ref, c_ref)
+        if c + 1 < chunks:
+            build(c + 1, *((a1_ref, c1_ref), (a0_ref, c0_ref))[c % 2])
+        if c == 2 * head:
+            kick()
+
     inverse = 1.0 / rho_ref[...]
     inv_ref[...] = inverse
-    sound_ref[...] = jnp.sqrt(ADIABATIC_INDEX * pressure * inverse)
-    lane = lax.broadcasted_iota(jnp.int32, (cx, cy, nz), 2)
-    after = jnp.where(lane == nz - 1, 0.0, pltpu.roll(pressure, nz - 1, 2))
-    before = jnp.where(lane == 0, 0.0, pltpu.roll(pressure, 1, 2))
-    half = 0.5 * KICK
-    imp_ref[2] -= half * (after - before)
-    line = lax.broadcasted_iota(jnp.int32, (cx, cy, nz), 1)
-    after = jnp.where(line == cy - 1, 0.0, pltpu.roll(pressure, cy - 1, 1))
-    before = jnp.where(line == 0, 0.0, pltpu.roll(pressure, 1, 1))
-    imp_ref[1] -= half * (after - before)
-    none = jnp.zeros((1, cy, nz), F32)
-    after = jnp.concatenate([pressure[1:], none], axis=0)
-    before = jnp.concatenate([none, pressure[:-1]], axis=0)
-    imp_ref[0] -= half * (after - before)
+    sound_ref[...] = jnp.sqrt(ADIABATIC_INDEX * (ADIABATIC_INDEX - 1.0) * en_ref[...] * inverse)
     arrive(*faces)
     imp_ref[0, 0] += half * in_face[0]
     imp_ref[0, cx - 1] -= half * in_face[1]
@@ -316,6 +326,15 @@
     wave = jnp.max(wave.reshape(cells, nz), axis=0, keepdims=True)
     top = functools.reduce(jnp.maximum, [wave[:, k * 128 : (k + 1) * 128] for k in range(nz // 128)])
 
+    def settle():
+        stays = col_ref[...] >= 0.0
+        state_ref[:, :rows] = jnp.where(stays, pay_ref[0:5, :], 0.0)
+        moved_ref[:, :rows] = jnp.where(stays, cell_ref[...], 0)
+        for b in range(4):
+            got = in_bucket[b]
+            state_ref[:, rows + b * cap : rows + (b + 1) * cap] = got[0:5]
+            moved_ref[:, rows + b * cap : rows + (b + 1) * cap] = got[5:8].astype(jnp.int32)
+
     def everyone(slots, sem):
         rest = slots.at[pl.ds(1, slots.shape[0] - 1)]
         return pltpu.make_async_copy(rest, rest, sem)
@@ -328,6 +347,8 @@
                 src_ref=slots.at[0], dst_ref=slots.at[k + 1], send_sem=max_send.at[t],
                 recv_sem=max_recv.at[t], device_id=peer(*p), device_id_type=MESH,
             ).start()
+        if t == 0:
+            settle()
         everyone(slots, max_recv.at[t]).wait()
         top = jnp.max(slots[...], axis=0)
     step_ref[...] = COURANT / jnp.broadcast_to(jnp.max(top, axis=1, keepdims=True), (1, 128))
@@ -366,9 +387,10 @@
             pltpu.VMEM((3, slots), jnp.int32),
             pltpu.VMEM((1, 128), F32),
         ),
-        in_specs=[pl.BlockSpec(memory_space=pltpu.SMEM)] + [pl.BlockSpec(memory_space=pltpu.HBM)] * 7,
+        in_specs=[pl.BlockSpec(memory_space=pltpu.HBM)] * 8,
         out_specs=(vmem,) * 6,
         scratch_shapes=[
+            pltpu.VMEM((128, 256), BF16),
             pltpu.VMEM((8, rows), F32),
             pltpu.VMEM((8, rows), F32),
             pltpu.VMEM((1, rows), F32),
@@ -393,11 +415,12 @@
             pltpu.SemaphoreType.DMA((4,)),
             pltpu.SemaphoreType.DMA((len(rounds),)),
             pltpu.SemaphoreType.DMA((len(rounds),)),
+            pltpu.SMEM((1,), jnp.int32),
             pltpu.VMEM((1, rows), F32),
             pltpu.VMEM(velocity.shape, F32),
             pltpu.VMEM((1, rows), F32),
             pltpu.VMEM(cell.shape, jnp.int32),
-            pltpu.SemaphoreType.DMA((7,)),
+            pltpu.SemaphoreType.DMA((8,)),
         ] + [pltpu.VMEM((len(group) + 1, 1, 128), F32) for group in rounds],
         compiler_params=pltpu.CompilerParams(
             collective_id=0, has_side_effects=True, vmem_limit_bytes=64200000
@@ -406,14 +429,14 @@
     )(count, density, momentum, energy, mass.reshape(1, rows), velocity, temp.reshape(1, rows), cell)
     final = pl.pallas_call(
         put_out,
-        out_shape=tuple(pltpu.HBM(o.shape, o.dtype) for o in outs[:5]),
-        in_specs=[vmem] * 5,
-        out_specs=(pl.BlockSpec(memory_space=pltpu.HBM),) * 5,
-        scratch_shapes=[pltpu.SemaphoreType.DMA((5,))],
+        out_shape=tuple(pltpu.HBM(o.shape, o.dtype) for o in outs),
+        in_specs=[vmem] * 6,
+        out_specs=(pl.BlockSpec(memory_space=pltpu.HBM),) * 6,
+        scratch_shapes=[pltpu.SemaphoreType.DMA((6,))],
         compiler_params=pltpu.CompilerParams(vmem_limit_bytes=8 * 1024 * 1024),
         name="put_out",
-    )(*outs[:5])
-    return tuple(final) + (outs[5][0, 0],)
+    )(*outs)
+    return tuple(final[:5]) + (final[5][0, 0],)
 
 
 def solution(mesh):

time: 27.1 us -> 25.6 us (0.945)
  between operations: 2.45 us -> 1.29 us
  Pallas kernels: 24.5 us -> 24.1 us
    pallas_call x1, Pallas kernels: 23.2 us -> 22.9 us  [on_device(): pl.pallas_call(functools.partial(kernel, n_gx, n_gy), out_shape=(pltpu.VM...]
where the time goes in v2:
time: 25.6 us; the launch traced here: 25.4 us
  Pallas kernels  24.1 us (94%)
  between operations  1.29 us (5%)
    pallas_call x1, Pallas kernels, on_device(): pl.pallas_call(functools.partial(kernel, n_gx, n_gy), out_shape=(pltpu.VM...  22.9 us
    pallas_call x1, Pallas kernels, on_device(): pl.pallas_call(put_out, out_shape=tuple((pltpu.HBM(o.shape, o.dtype) for...  1.26 us

profile of v2, /device:TPU:0, one launch (start us, length us, event | category | flops | bytes accessed | tf_op | source)
XLA Modules:
  0.0 25.4 jit_solution(10109481463401211519)
XLA Ops:
  1.3 22.9 %spray.1 = (f32[16,16,256]{2,1,0:T(8,128)S(1)}, f32[3,16,16,256]{3,2,1,0:T(8,128)S(1)}, f32[16,16,256]{2,1,0:T(8,128)S(1)}, f32[5,10240]{1,0:T(8,128)S(1)}, s32[...) custom-call(s32[1]{0:T(128)S(6)} %copy.14.count_hbm, f32[16,16,256]{2,1,0:T(8,128)} %density_hbm.1, ...), custom_call_target="tpu_custom_call" | custom-call | tf_op jit(solution)/shard_map/spray/pallas_call | solution.py:380
  24.1 1.3 %put_out.1 = (f32[16,16,256]{2,1,0:T(8,128)}, f32[3,16,16,256]{3,2,1,0:T(8,128)}, f32[16,16,256]{2,1,0:T(8,128)}, f32[5,10240]{1,0:T(8,128)}, s32[3,10240]{1,0:T(4,128)}, /*index=5*/f32[1,128]{1,0:T(1,128)}) custom-call(f32[16,16,256]{2,1,0:T(8,128)S(1)} %get-tuple-element.18.refs_0_, f32[3,16,16,256]{3,2,1,0:T(8,128)S(1)} %get-tuple-element.19.refs_1_, ...), custom_call_target="tpu_custom_call" | custom-call | tf_op jit(solution)/shard_map/put_out/pallas_call | solution.py:430

commit v3 on v2

--- a/solution.py
+++ b/solution.py
@@ -30,20 +30,21 @@
     return high, low
 
 
-def one_hot_rows(row, count):
+def one_hot_rows(row, count, hot=1.0):
     lanes = row.shape[1]
     base = (
         jnp.broadcast_to(row, (16, lanes))
         - lax.broadcasted_iota(jnp.int32, (16, lanes), 0).astype(F32)
     ).astype(BF16)
-    one, zero = jnp.ones((16, lanes), BF16), jnp.zeros((16, lanes), BF16)
+    one, zero = jnp.full((16, lanes), hot, BF16), jnp.zeros((16, lanes), BF16)
     return jnp.concatenate(
         [jnp.where(base == 16.0 * k, one, zero) for k in range(count // 16)], axis=0
     )
 
 
 def peers_of(n_gx, n_gy):
-    both = [(a, b) for a in range(n_gx) for b in range(n_gy) if a or b]
+    both = [(a, b) for b in range(n_gy) for a in range(n_gx) if a or b]
+    both = both[n_gx - 1 :] + both[: n_gx - 1]
     if n_gx * n_gy <= 64:
         return (both,)
     return ([p for p in both if p[1] == 0], [p for p in both if p[0] == 0])
@@ -71,6 +72,9 @@
     per = cap // 128
     cells = cx * cy
     chunks = rows // CHUNK
+    i0 = lax.broadcasted_iota(jnp.int32, (128, 256), 0)
+    i1 = lax.broadcasted_iota(jnp.int32, (128, 256), 1)
+    upper_ref[...] = jnp.where((i0 < i1) | (i1 >= 128), 1.0, 0.0).astype(BF16)
     in_bucket[...] = jnp.zeros_like(in_bucket)
     in_face[...] = jnp.zeros_like(in_face)
 
@@ -86,22 +90,19 @@
     for load in loads[:5]:
         load.wait()
     blocks = CHUNK // 128
-    i0 = lax.broadcasted_iota(jnp.int32, (128, 256), 0)
-    i1 = lax.broadcasted_iota(jnp.int32, (128, 256), 1)
-    upper_ref[...] = jnp.where((i0 < i1) | (i1 >= 128), 1.0, 0.0).astype(BF16)
 
     def prepare(c, carry):
         lanes = pl.ds(c * CHUNK, CHUNK)
         mass, temp = mass_ref[:, lanes], temp_ref[:, lanes]
         live = lax.broadcasted_iota(jnp.int32, (1, CHUNK), 1) + c * CHUNK < count_ref[0]
-        evap = jnp.where(live, mass * jax.nn.sigmoid(2.0 * (temp - 2.0)), 0.0)
+        evap = jnp.where(live, LIFT * (mass * jax.nn.sigmoid(2.0 * (temp - 2.0))), 0.0)
         vx, vy, vz = vel_ref[0:1, lanes], vel_ref[1:2, lanes], vel_ref[2:3, lanes]
         src_ref[0:1, lanes] = evap
         src_ref[1:2, lanes] = evap * vx
         src_ref[2:3, lanes] = evap * vy
         src_ref[3:4, lanes] = evap * vz
         src_ref[4:5, lanes] = evap * (temp + 0.5 * (vx * vx + vy * vy + vz * vz))
-        pay_ref[0:1, lanes] = mass - SHRINK * evap
+        pay_ref[0:1, lanes] = mass - (SHRINK / LIFT) * evap
         pay_ref[1:4, lanes] = vel_ref[:, lanes]
         pay_ref[4:5, lanes] = temp
         pay_ref[5:8, lanes] = cell_ref[:, lanes].astype(F32)
@@ -142,7 +143,7 @@
         zero = jnp.zeros((16, CHUNK), BF16)
         value = jnp.broadcast_to(src_ref[v : v + 1, lanes], (16, CHUNK))
         high = value.astype(BF16)
-        low = ((value - high.astype(F32)) * LIFT).astype(BF16)
+        low = (value - high.astype(F32)).astype(BF16)
         first = [jnp.where(hits[k], high, zero) for k in range(cells // 16)]
         second = [
             jnp.concatenate([jnp.where(hits[k], low, zero), jnp.where(hits[k + 1], low, zero)], axis=0).astype(F8)
@@ -158,8 +159,8 @@
         zero = jnp.zeros((16, CHUNK), BF16)
         left = jnp.concatenate([jnp.where(q == float(k), both, zero) for k in range(groups)], axis=0)
         small_ref[...] += dot_nt(left, one_hot_rows(r_ref[:, lanes], 128))
-        depth = one_hot_rows(cell_ref[2:3, lanes].astype(F32), nz)
-        unit = (depth * (1.0 / LIFT)).astype(F8)
+        depth = one_hot_rows(cell_ref[2:3, lanes].astype(F32), nz, 1.0 / LIFT)
+        unit = depth.astype(F8)
         b_ref[c] = depth
         d_ref[c] = unit
         first, second = spread(4, lanes, columns(lanes))
@@ -327,6 +328,8 @@
     top = functools.reduce(jnp.maximum, [wave[:, k * 128 : (k + 1) * 128] for k in range(nz // 128)])
 
     def settle():
+        depart(*moves)
+        depart(*faces)
         stays = col_ref[...] >= 0.0
         state_ref[:, :rows] = jnp.where(stays, pay_ref[0:5, :], 0.0)
         moved_ref[:, :rows] = jnp.where(stays, cell_ref[...], 0)
@@ -352,8 +355,6 @@
         everyone(slots, max_recv.at[t]).wait()
         top = jnp.max(slots[...], axis=0)
     step_ref[...] = COURANT / jnp.broadcast_to(jnp.max(top, axis=1, keepdims=True), (1, 128))
-    depart(*moves)
-    depart(*faces)
     for t in range(len(rounds)):
         everyone(slots_refs[t], max_send.at[t]).wait()
 

time: 25.6 us -> 25.5 us (level)
  no operation moved by 1% of the time
where the time goes in v3:
time: 25.5 us; the launch traced here: 25.3 us
  Pallas kernels  24 us (94%)
  between operations  1.29 us (5%)
    pallas_call x1, Pallas kernels, on_device(): pl.pallas_call(functools.partial(kernel, n_gx, n_gy), out_shape=(pltpu.VM...  22.8 us
    pallas_call x1, Pallas kernels, on_device(): pl.pallas_call(put_out, out_shape=tuple((pltpu.HBM(o.shape, o.dtype) for...  1.26 us

profile of v3, /device:TPU:0, one launch (start us, length us, event | category | flops | bytes accessed | tf_op | source)
XLA Modules:
  0.0 25.3 jit_solution(6980393413812317232)
XLA Ops:
  1.3 22.8 %spray.1 = (f32[16,16,256]{2,1,0:T(8,128)S(1)}, f32[3,16,16,256]{3,2,1,0:T(8,128)S(1)}, f32[16,16,256]{2,1,0:T(8,128)S(1)}, f32[5,10240]{1,0:T(8,128)S(1)}, s32[...) custom-call(s32[1]{0:T(128)S(6)} %copy.14.count_hbm, f32[16,16,256]{2,1,0:T(8,128)} %density_hbm.1, ...), custom_call_target="tpu_custom_call" | custom-call | tf_op jit(solution)/shard_map/spray/pallas_call | solution.py:381
  24.1 1.3 %put_out.1 = (f32[16,16,256]{2,1,0:T(8,128)}, f32[3,16,16,256]{3,2,1,0:T(8,128)}, f32[16,16,256]{2,1,0:T(8,128)}, f32[5,10240]{1,0:T(8,128)}, s32[3,10240]{1,0:T(4,128)}, /*index=5*/f32[1,128]{1,0:T(1,128)}) custom-call(f32[16,16,256]{2,1,0:T(8,128)S(1)} %get-tuple-element.18.refs_0_, f32[3,16,16,256]{3,2,1,0:T(8,128)S(1)} %get-tuple-element.19.refs_1_, ...), custom_call_target="tpu_custom_call" | custom-call | tf_op jit(solution)/shard_map/put_out/pallas_call | solution.py:431
